TPU v7x, 32 devices: a whole 2x2x4 slice. The times are simulated.
32 devices in a mesh: dp: 4 (over x, core), row: 2 (over y), col: 4 (over z).
Axes of the slice: x: 2, y: 2, z: 4, core: 2. Of those that a mesh axis runs over, the one named last changes fastest.
Arguments:
- act_in: bfloat16 [4096, 2304], P(('dp', 'row'), 'col'), may hold values from -6 to 6
- cot_out: bfloat16 [4096, 2304], P(('dp', 'row'), 'col'), may hold values from -6 to 6
- w_gate: bfloat16 [2304, 4608], P(('dp', 'row'), 'col'), may hold values from -0.125 to 0.125
- w_up: bfloat16 [2304, 4608], P(('dp', 'row'), 'col'), may hold values from -0.125 to 0.125
- w_down: bfloat16 [4608, 2304], P('col', ('dp', 'row')), may hold values from -0.09375 to 0.09375
Outputs:
- input_grad: bfloat16 [4096, 2304], P(('dp', 'row'), 'col')
- gate_grad: float32 [2304, 4608], P(('dp', 'row'), 'col')
- up_grad: float32 [2304, 4608], P(('dp', 'row'), 'col')
- down_grad: float32 [4608, 2304], P('col', ('dp', 'row'))
All inputs are finite; a program needn't handle non-finite values.
Results may differ from a plain program's by a relative error of at most 0.015.
Values may be sent and summed in bfloat16 or wider, within the bound.
No kernel may reach another device: no remote copies, remote signals or barrier semaphores. Data moves between devices by JAX's collectives and lax.ppermute only.
A program may use at most 128 MiB of HBM per device.

v0:
```python
import math
import jax
import jax.numpy as jnp
from jax import lax
from jax.sharding import PartitionSpec as P

gelu_cubic = 0.044715
gelu_scale = 0.7978845608028654


def gelu_parts(values):
    inner_arg = gelu_scale * (values + gelu_cubic * values * values * values)
    tanh_val = jnp.tanh(inner_arg)
    output = 0.5 * values * (1.0 + tanh_val)
    slope_val = 0.5 * (1.0 + tanh_val) + 0.5 * values * (1.0 - tanh_val * tanh_val) * gelu_scale * (
        1.0 + 3.0 * gelu_cubic * values * values
    )
    return (output, slope_val)


def token_contract(left, right):
    return lax.dot_general(
        left, right, (((0,), (0,)), ((), ())), preferred_element_type=jnp.float32
    )


def body(act_in, cot_out, w_gate, w_up, w_down):
    tok_rows = act_in.shape[0]
    hid_cols = w_gate.shape[1]
    act_full, cot_full = (
        lax.all_gather(act_in, "col", axis=1, tiled=True),
        lax.all_gather(cot_out, "col", axis=1, tiled=True),
    )
    gate_cols, up_cols = (
        lax.all_gather(w_gate, ("dp", "row"), axis=0, tiled=True),
        lax.all_gather(w_up, ("dp", "row"), axis=0, tiled=True),
    )
    gate_pre = jnp.dot(act_full, gate_cols, preferred_element_type=jnp.float32)
    up_pre = jnp.dot(act_full, up_cols, preferred_element_type=jnp.float32)
    cot_block = cot_full
    hidden_grad = lax.dot_general(
        cot_block,
        lax.all_gather(w_down, ("dp", "row"), axis=1, tiled=True),
        (((1,), (1,)), ((), ())),
        preferred_element_type=jnp.float32,
    )
    act_val, slope_val = gelu_parts(gate_pre)
    hidden = (act_val * up_pre).astype(jnp.bfloat16)
    d_gate = (hidden_grad * up_pre * slope_val).astype(jnp.bfloat16)
    d_up = (hidden_grad * act_val).astype(jnp.bfloat16)
    feature_dims = (((1,), (1,)), ((), ()))
    part_sum = lax.dot_general(d_gate, gate_cols, feature_dims, preferred_element_type=jnp.float32)
    part_sum = part_sum + lax.dot_general(
        d_up, up_cols, feature_dims, preferred_element_type=jnp.float32
    )
    rounded = lax.optimization_barrier(part_sum.astype(jnp.bfloat16)).astype(jnp.float32)
    input_grad = lax.psum_scatter(
        rounded.astype(jnp.bfloat16), "col", scatter_dimension=1, tiled=True
    )
    norm_scale = 1.0 / math.sqrt(tok_rows * lax.axis_size(("dp", "row")))
    cot_block = cot_full
    shares = lax.psum_scatter(
        jnp.concatenate(
            [
                token_contract(act_full, d_gate),
                token_contract(act_full, d_up),
                token_contract(cot_block, hidden),
            ],
            axis=1,
        ).astype(jnp.bfloat16),
        ("dp", "row"),
        scatter_dimension=0,
        tiled=True,
    ).astype(jnp.float32)
    gate_grad = shares[:, :hid_cols] * norm_scale
    up_grad = shares[:, hid_cols : 2 * hid_cols] * norm_scale
    down_grad = shares[:, 2 * hid_cols :].T * norm_scale
    return (input_grad, gate_grad, up_grad, down_grad)


def solution(mesh):
    placed = (
        P(("dp", "row"), "col"),
        P(("dp", "row"), "col"),
        P(("dp", "row"), "col"),
        P(("dp", "row"), "col"),
        P("col", ("dp", "row")),
    )
    return jax.shard_map(
        body,
        mesh=mesh,
        in_specs=placed,
        out_specs=(
            P(("dp", "row"), "col"),
            P(("dp", "row"), "col"),
            P(("dp", "row"), "col"),
            P("col", ("dp", "row")),
        ),
        check_vma=False,
    )
```

profile of v0, /device:TPU:0, one launch (start us, length us, event | category | flops | bytes accessed | tf_op | source)
XLA Modules:
  0.0 470.1 jit_solution(8092065288769232010)
XLA Ops:
  7.2 0.0 all-gather.10.cloned.1.call-start
  7.2 0.7 all-gather.10.cloned.1.call-update
  7.9 0.0 all-gather.12.cloned.1.call-start
  7.9 0.7 all-gather.12.cloned.1.call-update
  8.6 0.0 all-gather.14.cloned.1.call-start
  8.7 0.7 all-gather.14.cloned.1.call-update
  9.4 0.0 all-gather.6.cloned.1.call-start
  9.4 0.5 all-gather.6.cloned.1.call-update
  10.0 0.0 all-gather.8.cloned.1.call-start
  10.0 0.5 all-gather.8.cloned.1.call-update
  10.5 0.0 reduce-scatter.9.cloned.1.call-start
  10.6 51.7 %all-gather.10.cloned.1.call-done = bf16[512,2304]{0,1:T(8,128)(2,1)} async-done(((bf16[512,576]{0,1:T(8,128)(2,1)}), bf16[512,2304]{0,1:T(8,128)(2,1)}) %all-gather.10.cloned.1.call-update) | async-done | bytes 2359312 | tf_op jit(solution)/shard_map/all_gather | solution.py:31
  62.3 0.0 copy-start
  62.3 41.9 %all-gather.12.cloned.1.call-done = bf16[2304,1152]{1,0:T(8,128)(2,1)} async-done(((bf16[288,1152]{1,0:T(8,128)(2,1)}), bf16[2304,1152]{1,0:T(8,128)(2,1)}) %all-gather.12.cloned.1.call-update) | async-done | bytes 5308432 | tf_op jit(solution)/shard_map/all_gather | solution.py:36
  104.2 7.9 %fusion.16 = f32[512,1152]{1,0:T(8,128)} fusion(bf16[512,2304]{0,1:T(8,128)(2,1)} %all-gather.10.cloned.1.call-done, bf16[2304,1152]{1,0:T(8,128)(2,1)} %all-gather.12.cloned.1.call-done), kind=kOutput, calls=%fused_computation.29 | convolution fusion | flops 2717908992 | bytes 10027008 | tf_op jit(solution)/shard_map/dot_general | solution.py:39
  112.1 35.3 %all-gather.14.cloned.1.call-done = bf16[2304,1152]{1,0:T(8,128)(2,1)} async-done(((bf16[288,1152]{1,0:T(8,128)(2,1)}), bf16[2304,1152]{1,0:T(8,128)(2,1)}) %all-gather.14.cloned.1.call-update) | async-done | bytes 5308432 | tf_op jit(solution)/shard_map/all_gather | solution.py:35
  147.4 0.0 copy-done
  147.4 7.2 %fusion.17 = f32[512,1152]{1,0:T(8,128)} fusion(bf16[512,2304]{0,1:T(8,128)(2,1)S(1)} %copy-done, bf16[2304,1152]{1,0:T(8,128)(2,1)} %all-gather.14.cloned.1.call-done), kind=kOutput, calls=%fused_computation.30 | convolution fusion | flops 2717908992 | bytes 10027008 | tf_op jit(solution)/shard_map/dot_general | solution.py:38
  154.6 44.2 %all-gather.6.cloned.1.call-done = bf16[512,2304]{0,1:T(8,128)(2,1)} async-done(((bf16[512,576]{0,1:T(8,128)(2,1)}), bf16[512,2304]{0,1:T(8,128)(2,1)}) %all-gather.6.cloned.1.call-update) | async-done | bytes 2359312 | tf_op jit(solution)/shard_map/all_gather | solution.py:32
  198.8 9.2 %fusion.2 = bf16[2304,1152]{0,1:T(8,128)(2,1)} fusion(bf16[512,2304]{0,1:T(8,128)(2,1)} %all-gather.6.cloned.1.call-done, f32[512,1152]{1,0:T(8,128)} %fusion.16, f32[512,1152]{1,0:T(8,128)} %fusion.17), kind=kOutput, calls=%fused_computation.6 | convolution fusion | flops 2726461440 | bytes 12386304 | tf_op jit(solution)/shard_map/dot_general | solution.py:22
  208.0 32.6 %all-gather.8.cloned.1.call-done = bf16[1152,2304]{0,1:T(8,128)(2,1)} async-done(((bf16[1152,288]{0,1:T(8,128)(2,1)}), bf16[1152,2304]{0,1:T(8,128)(2,1)}) %all-gather.8.cloned.1.call-update) | async-done | bytes 5308432 | tf_op jit(solution)/shard_map/all_gather | solution.py:43
  240.6 9.5 %multiply_convert_fusion.1 = (bf16[512,1152]{1,0:T(8,128)(2,1)S(1)}, bf16[512,1152]{1,0:T(8,128)(2,1)S(1)}) fusion(f32[512,1152]{1,0:T(8,128)} %fusion.17, f32[512,1152]{1,0:T(8,128)} %fusion.16, bf16[512,2304]{0,1:T(8,128)(2,1)} %all-gather.6.cloned.1.call-done, bf16[1152,2304]{0,1:T(8,128)(2,1)} %all-gather.8.cloned.1.call-done), kind=kOutput, calls=%fused_computation.19 | convolution fusion | flops 2731474944 | bytes 14745600 | tf_op jit(solution)/shard_map/dot_general | solution.py:41
  250.1 0.0 copy-start.1
  250.1 0.0 slice-start
  250.1 3.5 fusion.1
  253.6 0.0 slice-start.1
  253.6 0.0 copy-done.1
  253.6 3.5 fusion
  257.2 0.0 slice-done
  257.2 0.0 slice-done.1
  257.2 23.7 %pad_maximum_fusion = bf16[2304,3456]{0,1:T(8,128)(2,1)} fusion(bf16[2304,1152]{0,1:T(8,128)(2,1)S(1)} %bitcast.28, bf16[2304,1152]{0,1:T(8,128)(2,1)S(1)} %fusion.1, bf16[2304,1152]{0,1:T(8,128)(2,1)S(1)} %fusion), kind=kLoop, calls=%fused_computation | loop fusion | flops 47775744 | bytes 31850496 | tf_op jit(solution)/shard_map/concatenate | solution.py:63
  280.9 20.3 %copy.19 = bf16[2304,3456]{1,0:T(8,128)(2,1)} copy(bf16[2304,3456]{0,1:T(8,128)(2,1)} %pad_maximum_fusion) | data formatting | bytes 31850496
  301.2 0.0 copy-start.2
  301.2 0.0 reduce-scatter.9.cloned.1.call-update
  301.3 0.3 reduce-scatter.7.cloned.1.call-start
  301.5 1.0 copy-done.2
  302.5 5.7 %fusion.18 = f32[512,2304]{1,0:T(8,128)S(1)} fusion(bf16[512,1152]{1,0:T(8,128)(2,1)S(1)} %copy-done.2, bf16[2304,1152]{1,0:T(8,128)(2,1)} %all-gather.14.cloned.1.call-done), kind=kOutput, calls=%fused_computation.31 | convolution fusion | flops 2717908992 | bytes 11206656 | tf_op jit(solution)/shard_map/dot_general | solution.py:52
  308.3 7.1 %fusion.3 = bf16[512,2304]{1,0:T(8,128)(2,1)S(1)} fusion(f32[512,2304]{1,0:T(8,128)S(1)} %fusion.18, bf16[512,1152]{1,0:T(8,128)(2,1)S(1)} %get-tuple-element.15, bf16[2304,1152]{1,0:T(8,128)(2,1)} %all-gather.12.cloned.1.call-done), kind=kOutput, calls=%fused_computation.8 | convolution fusion | flops 2720268288 | bytes 13565952 | tf_op jit(solution)/shard_map/dot_general | solution.py:53
  315.4 2.5 copy.17
  317.9 0.0 reduce-scatter.7.cloned.1.call-update
  317.9 94.8 %reduce-scatter.9.cloned.1.call-done = bf16[288,3456]{1,0:T(8,128)(2,1)} async-done(((bf16[2304,3456]{1,0:T(8,128)(2,1)}), bf16[288,3456]{1,0:T(8,128)(2,1)}) %reduce-scatter.9.cloned.1.call-update) | async-done | bytes 1990672
  412.7 3.0 copy.20
  415.7 0.3 convert_element_type.22
  416.0 1.6 fusion.11
  417.6 3.0 copy.16
  420.6 1.6 copy.15
  422.2 1.6 copy.14
  423.8 39.5 %reduce-scatter.7.cloned.1.call-done = bf16[576,512]{1,0:T(8,128)(2,1)} async-done(((bf16[2304,512]{1,0:T(8,128)(2,1)}), bf16[576,512]{1,0:T(8,128)(2,1)}) %reduce-scatter.7.cloned.1.call-update) | async-done | bytes 589840
  (1 shorter events, 0.0 us)
Async XLA Ops:
  7.2 55.1 %all-gather.10.cloned.1.call-start = ((), (), s32[]{:S(2)}) async-start(), calls=%async_computation.4 | async-start | bytes 2949120 | tf_op jit(solution)/shard_map/all_gather | solution.py:31
  7.9 96.3 %all-gather.12.cloned.1.call-start = ((), (), s32[]{:S(2)}) async-start(), calls=%async_computation.5 | async-start | bytes 5971968 | tf_op jit(solution)/shard_map/all_gather | solution.py:36
  8.6 138.7 %all-gather.14.cloned.1.call-start = ((), (), s32[]{:S(2)}) async-start(), calls=%async_computation.6 | async-start | bytes 5971968 | tf_op jit(solution)/shard_map/all_gather | solution.py:35
  9.4 189.4 %all-gather.6.cloned.1.call-start = ((), (), s32[]{:S(2)}) async-start(), calls=%async_computation.2 | async-start | bytes 2949120 | tf_op jit(solution)/shard_map/all_gather | solution.py:32
  10.0 230.6 %all-gather.8.cloned.1.call-start = ((), (), s32[]{:S(2)}) async-start(), calls=%async_computation.3 | async-start | bytes 5971968 | tf_op jit(solution)/shard_map/all_gather | solution.py:43
  10.5 402.1 %reduce-scatter.9.cloned.1.call-start = ((), (), s32[]{:S(2)}) async-start(), calls=%async_computation.8 | async-start | bytes 17915904
  62.3 85.1 %copy-start = (bf16[512,2304]{0,1:T(8,128)(2,1)S(1)}, bf16[512,2304]{0,1:T(8,128)(2,1)}, u32[]{:S(2)}) copy-start(bf16[512,2304]{0,1:T(8,128)(2,1)} %all-gather.10.cloned.1.call-done) | copy-start | bytes 7077892
  250.1 3.6 copy-start.1
  250.1 7.1 %slice-start = ((s8[5308416]{0:T(1024)(128)(4,1)}), s8[4194304]{0:T(1024)(128)(4,1)S(1)}, s32[]{:S(2)}) async-start(s8[5308416]{0:T(1024)(128)(4,1)} %bitcast.27), calls=%async_computation.9 | async-start | bytes 8388608
  253.6 3.6 slice-start.1
  301.2 1.3 copy-start.2
  301.3 162.0 %reduce-scatter.7.cloned.1.call-start = ((), (), s32[]{:S(2)}) async-start(), calls=%async_computation.7 | async-start | bytes 2949120
Sparse Core Ops, SparseCore 0:
  9.5 52.6 all-gather.9
  64.2 40.0 all-gather.11
  106.1 41.2 all-gather.13
  148.8 49.9 all-gather.5
  200.5 40.0 all-gather.7
  301.4 111.2 reduce-scatter.8
  415.5 47.6 reduce-scatter.6
where the time goes:
time: 471 us; the launch traced here: 470 us
  waiting for transfers between devices  343 us (73%)
  matrix products  53.6 us (11%)
  local copies, waits for them, and re-layouts  33 us (7%)
  other arithmetic  25.6 us (5%)
  between operations  14.2 us (3%)
    unnamed x9, waiting for transfers between devices  137 us
    all_gather x1, waiting for transfers between devices, body(): lax.all_gather(act_in, 'col', axis=1, tiled=True)  51.7 us
    all_gather x1, waiting for transfers between devices, body(): lax.all_gather(cot_out, 'col', axis=1, tiled=True)  44.2 us
    all_gather x1, waiting for transfers between devices, body(): lax.all_gather(w_up, ('dp', 'row'), axis=0, tiled=True)  41.9 us
    all_gather x1, waiting for transfers between devices, body(): lax.all_gather(w_gate, ('dp', 'row'), axis=0, tiled=True)  35.3 us
    unnamed x16, local copies, waits for them, and re-layouts  33 us
    all_gather x1, waiting for transfers between devices, body(): lax.all_gather(w_down, ('dp', 'row'), axis=1, tiled=True)  32.6 us
    concatenate x1, other arithmetic, body(): jnp.concatenate([token_contract(act_full, d_gate), token_contract(act_ful...  23.7 us
  transfers between devices with their start and end apart: 7, of which 7 were waited for; matrix products, arithmetic and copies ran while one was open for 11% of the time, Pallas kernels for 0%

commit v1 on v0

--- a/solution.py
+++ b/solution.py
@@ -1,3 +1,4 @@
+import functools
 import math
 import jax
 import jax.numpy as jnp
@@ -6,6 +7,23 @@
 
 gelu_cubic = 0.044715
 gelu_scale = 0.7978845608028654
+
+
+def meet_stocks(my_data, axis_no):
+    u_next = lax.psum(1, axis_name=("dp", "row"))
+    step_out = lax.axis_index(("dp", "row"))
+    last, odd, outcome_arr = (u_next, step_out, my_data.shape[axis_no])
+    moved, mat_out = (my_data, 1)
+    while mat_out < last:
+        answer = lax.ppermute(
+            moved, axis_name=("dp", "row"), perm=[(jj, (jj - mat_out) % last) for jj in range(last)]
+        )
+        moved = jnp.concatenate([moved, answer], axis=axis_no)
+        mat_out = 2 * mat_out
+    return jnp.roll(moved, odd * outcome_arr, axis=axis_no)
+
+
+start_masks = functools.partial(meet_stocks, axis_no=1)
 
 
 def gelu_parts(values):
@@ -39,10 +57,7 @@
     up_pre = jnp.dot(act_full, up_cols, preferred_element_type=jnp.float32)
     cot_block = cot_full
     hidden_grad = lax.dot_general(
-        cot_block,
-        lax.all_gather(w_down, ("dp", "row"), axis=1, tiled=True),
-        (((1,), (1,)), ((), ())),
-        preferred_element_type=jnp.float32,
+        cot_block, start_masks(w_down), (((1,), (1,)), ((), ())), preferred_element_type=jnp.float32
     )
     act_val, slope_val = gelu_parts(gate_pre)
     hidden = (act_val * up_pre).astype(jnp.bfloat16)

time: 471 us -> 453 us (0.962)
  waiting for transfers between devices: 343 us -> 310 us
  local copies, waits for them, and re-layouts: 33 us -> 46.2 us
  matrix products: 53.6 us -> 48 us
  starting transfers between devices: 0.49 us -> 5.65 us
    ppermute x0 -> x3, waiting for transfers between devices: none -> 108 us  [meet_stocks(): lax.ppermute(moved, axis_name=('dp', 'row'), perm=[(jj, (jj - mat_out) %...]
    all_gather x1, waiting for transfers between devices: 51.7 us -> 0.01 us  [body(): lax.all_gather(act_in, 'col', axis=1, tiled=True)]
    all_gather x1, waiting for transfers between devices: 41.9 us -> 0.01 us  [body(): lax.all_gather(w_up, ('dp', 'row'), axis=0, tiled=True)]
    all_gather x1 -> x0, waiting for transfers between devices: 32.6 us -> none  [body(): lax.all_gather(w_down, ('dp', 'row'), axis=1, tiled=True)]
    all_gather x1, waiting for transfers between devices: 35.3 us -> 22.7 us  [body(): lax.all_gather(w_gate, ('dp', 'row'), axis=0, tiled=True)]
    unnamed x16 -> x27, local copies, waits for them, and re-layouts: 33 us -> 42.5 us
    ppermute x0 -> x3, starting transfers between devices: none -> 5.19 us  [meet_stocks(): lax.ppermute(moved, axis_name=('dp', 'row'), perm=[(jj, (jj - mat_out) %...]
    unnamed x9 -> x8, waiting for transfers between devices: 137 us -> 135 us
  transfers between devices with their start and end apart: 7 -> 9, of which waited for: 7 -> 7; matrix products, arithmetic and copies ran while one was open for 11% -> 12% of each run, Pallas kernels for 0% -> 0%
where the time goes in v1:
time: 453 us; the launch traced here: 452 us
  waiting for transfers between devices  310 us (68%)
  matrix products  48 us (11%)
  local copies, waits for them, and re-layouts  46.2 us (10%)
  other arithmetic  27.4 us (6%)
  between operations  14.3 us (3%)
  starting transfers between devices  5.65 us (1%)
    unnamed x8, waiting for transfers between devices  135 us
    ppermute x3, waiting for transfers between devices, meet_stocks(): lax.ppermute(moved, axis_name=('dp', 'row'), perm=[(jj, (jj - mat_out) %...  108 us
    all_gather x1, waiting for transfers between devices, body(): lax.all_gather(cot_out, 'col', axis=1, tiled=True)  44.6 us
    unnamed x27, local copies, waits for them, and re-layouts  42.5 us
    concatenate x1, other arithmetic, body(): jnp.concatenate([token_contract(act_full, d_gate), token_contract(act_ful...  23.7 us
    all_gather x1, waiting for transfers between devices, body(): lax.all_gather(w_gate, ('dp', 'row'), axis=0, tiled=True)  22.7 us
    dot_general x3, matrix products, token_contract(): lax.dot_general(left, right, (((0,), (0,)), ((), ())), preferred_element_...  13.1 us
  transfers between devices with their start and end apart: 9, of which 7 were waited for; matrix products, arithmetic and copies ran while one was open for 12% of the time, Pallas kernels for 0%

profile of v1, /device:TPU:0, one launch (start us, length us, event | category | flops | bytes accessed | tf_op | source)
XLA Modules:
  0.0 451.6 jit_solution(10420995049833482231)
XLA Ops:
  7.2 0.0 copy-start
  7.2 0.0 all-gather.7.cloned.1.call-start
  7.2 0.7 all-gather.7.cloned.1.call-update
  7.9 0.0 all-gather.9.cloned.1.call-start
  8.0 0.7 all-gather.9.cloned.1.call-update
  8.7 0.0 all-gather.11.cloned.1.call-start
  8.7 0.7 all-gather.11.cloned.1.call-update
  9.4 0.0 all-gather.5.cloned.1.call-start
  9.4 3.4 collective-permute-start
  12.9 14.8 %collective-permute-done = bf16[1152,288]{0,1:T(8,128)(2,1)S(1)} collective-permute-done((bf16[1152,288]{0,1:T(8,128)(2,1)}, bf16[1152,288]{0,1:T(8,128)(2,1)S(1)}, u32[]{:S(2)}, u32[]{:S(2)}) %collective-permute-start) | collective-permute-done | bytes 663584 | tf_op jit(solution)/shard_map/ppermute | solution.py:18
  27.6 0.0 copy-done
  27.6 0.1 pad_maximum_fusion.2
  27.7 1.2 collective-permute-start.1
  28.9 15.3 %collective-permute-done.1 = bf16[1152,576]{0,1:T(8,128)(2,1)S(1)} collective-permute-done((bf16[1152,576]{0,1:T(8,128)(2,1)S(1)}, bf16[1152,576]{0,1:T(8,128)(2,1)S(1)}, u32[]{:S(2)}, u32[]{:S(2)}) %collective-permute-start.1) | collective-permute-done | bytes 1327136 | tf_op jit(solution)/shard_map/ppermute | solution.py:18
  44.2 1.7 pad_maximum_fusion.1
  45.9 0.6 collective-permute-start.2
  46.5 0.0 all-gather.5.cloned.1.call-update
  46.5 0.0 reduce-scatter.9.cloned.1.call-start
  46.6 0.9 constant_dynamic-update-slice_fusion.7
  47.5 0.9 constant_dynamic-update-slice_fusion.6
  48.4 1.2 constant_dynamic-update-slice_fusion.5
  49.6 78.1 %collective-permute-done.2 = bf16[1152,1152]{0,1:T(8,128)(2,1)} collective-permute-done((bf16[1152,1152]{0,1:T(8,128)(2,1)}, bf16[1152,1152]{0,1:T(8,128)(2,1)}, u32[]{:S(2)}, u32[]{:S(2)}) %collective-permute-start.2) | collective-permute-done | bytes 2654240 | tf_op jit(solution)/shard_map/ppermute | solution.py:18
  127.7 3.5 constant_dynamic-update-slice_fusion.4
  131.2 0.9 constant_dynamic-update-slice_fusion.3
  132.1 0.9 constant_dynamic-update-slice_fusion.2
  133.0 1.2 constant_dynamic-update-slice_fusion.1
  134.2 3.7 constant_dynamic-update-slice_fusion
  137.9 0.0 all-gather.7.cloned.1.call-done
  137.9 0.0 all-gather.9.cloned.1.call-done
  137.9 7.8 %fusion.22 = f32[512,1152]{0,1:T(8,128)} fusion(bf16[512,2304]{0,1:T(8,128)(2,1)} %all-gather.7.cloned.1.call-done, bf16[2304,1152]{1,0:T(8,128)(2,1)} %all-gather.9.cloned.1.call-done), kind=kOutput, calls=%fused_computation.43 | convolution fusion | flops 2717908992 | bytes 10027008 | tf_op jit(solution)/shard_map/dot_general | solution.py:57
  145.7 22.7 %all-gather.11.cloned.1.call-done = bf16[2304,1152]{1,0:T(8,128)(2,1)} async-done(((bf16[288,1152]{1,0:T(8,128)(2,1)}), bf16[2304,1152]{1,0:T(8,128)(2,1)}) %all-gather.11.cloned.1.call-update) | async-done | bytes 5308432 | tf_op jit(solution)/shard_map/all_gather | solution.py:53
  168.4 0.0 copy-done.1
  168.4 6.8 %fusion.23 = f32[512,1152]{0,1:T(8,128)} fusion(bf16[512,2304]{0,1:T(8,128)(2,1)S(1)} %copy-done.1, bf16[2304,1152]{1,0:T(8,128)(2,1)} %all-gather.11.cloned.1.call-done), kind=kOutput, calls=%fused_computation.44 | convolution fusion | flops 2717908992 | bytes 10027008 | tf_op jit(solution)/shard_map/dot_general | solution.py:56
  175.3 44.6 %all-gather.5.cloned.1.call-done = bf16[512,2304]{0,1:T(8,128)(2,1)} async-done(((bf16[512,576]{0,1:T(8,128)(2,1)}), bf16[512,2304]{0,1:T(8,128)(2,1)}) %all-gather.5.cloned.1.call-update) | async-done | bytes 2359312 | tf_op jit(solution)/shard_map/all_gather | solution.py:50
  219.8 0.0 copy-start.2
  219.8 0.0 copy-start.3
  219.8 0.0 copy-start.4
  219.8 6.7 %fusion.2 = bf16[2304,1152]{0,1:T(8,128)(2,1)S(1)} fusion(bf16[512,2304]{0,1:T(8,128)(2,1)} %all-gather.5.cloned.1.call-done, f32[512,1152]{0,1:T(8,128)} %fusion.22, f32[512,1152]{0,1:T(8,128)} %fusion.23), kind=kOutput, calls=%fused_computation.6 | convolution fusion | flops 2726461440 | bytes 12386304 | tf_op jit(solution)/shard_map/dot_general | solution.py:40
  226.6 0.0 copy-done.2
  226.6 0.0 copy-done.3
  226.6 0.0 copy-done.4
  226.6 7.2 %multiply_convert_fusion.1 = (bf16[512,1152]{0,1:T(8,128)(2,1)S(1)}, bf16[512,1152]{0,1:T(8,128)(2,1)S(1)}) fusion(f32[512,1152]{0,1:T(8,128)S(1)} %copy-done.4, f32[512,1152]{0,1:T(8,128)S(1)} %copy-done.3, bf16[512,2304]{0,1:T(8,128)(2,1)S(1)} %copy-done.2, bf16[1152,4608]{0,1:T(8,128)(2,1)} %constant_dynamic-update-slice_fusion, s32[]{:T(128)S(6)} %select_n.14), kind=kOutput, calls=%fused_computation.23 | convolution fusion | flops 2731474944 | bytes 14745604 | tf_op jit(solution)/shard_map/dot_general | solution.py:59
  233.8 0.0 copy-start.5
  233.8 3.2 fusion
  237.0 0.0 copy-done.5
  237.0 3.2 fusion.1
  240.2 23.7 %pad_maximum_fusion = bf16[2304,3456]{0,1:T(8,128)(2,1)} fusion(bf16[2304,1152]{0,1:T(8,128)(2,1)S(1)} %fusion.2, bf16[2304,1152]{0,1:T(8,128)(2,1)S(1)} %fusion.1, bf16[2304,1152]{0,1:T(8,128)(2,1)S(1)} %fusion), kind=kLoop, calls=%fused_computation | loop fusion | flops 47775744 | bytes 31850496 | tf_op jit(solution)/shard_map/concatenate | solution.py:78
  263.9 20.3 %copy.39 = bf16[2304,3456]{1,0:T(8,128)(2,1)} copy(bf16[2304,3456]{0,1:T(8,128)(2,1)} %pad_maximum_fusion) | data formatting | bytes 31850496
  284.2 0.0 copy-start.6
  284.2 0.0 reduce-scatter.9.cloned.1.call-update
  284.3 0.3 reduce-scatter.7.cloned.1.call-start
  284.5 1.0 copy-done.6
  285.5 5.8 %fusion.24 = f32[512,2304]{1,0:T(8,128)S(1)} fusion(bf16[512,1152]{0,1:T(8,128)(2,1)S(1)} %copy-done.6, bf16[2304,1152]{1,0:T(8,128)(2,1)} %all-gather.11.cloned.1.call-done), kind=kOutput, calls=%fused_computation.45 | convolution fusion | flops 2717908992 | bytes 11206656 | tf_op jit(solution)/shard_map/dot_general | solution.py:67
  291.3 7.3 %fusion.5 = bf16[512,2304]{1,0:T(8,128)(2,1)S(1)} fusion(f32[512,2304]{1,0:T(8,128)S(1)} %fusion.24, bf16[512,1152]{0,1:T(8,128)(2,1)S(1)} %get-tuple-element.15, bf16[2304,1152]{1,0:T(8,128)(2,1)} %all-gather.9.cloned.1.call-done), kind=kOutput, calls=%fused_computation.10 | convolution fusion | flops 2720268288 | bytes 13565952 | tf_op jit(solution)/shard_map/dot_general | solution.py:68
  298.5 2.5 copy.37
  301.0 0.0 reduce-scatter.7.cloned.1.call-update
  301.1 93.2 %reduce-scatter.9.cloned.1.call-done = bf16[288,3456]{1,0:T(8,128)(2,1)} async-done(((bf16[2304,3456]{1,0:T(8,128)(2,1)}), bf16[288,3456]{1,0:T(8,128)(2,1)}) %reduce-scatter.9.cloned.1.call-update) | async-done | bytes 1990672
  394.3 3.0 copy.40
  397.3 0.3 convert_element_type.22
  397.6 1.6 fusion.16
  399.2 3.0 copy.32
  402.3 1.6 copy.33
  403.8 1.6 copy.34
  405.4 39.3 %reduce-scatter.7.cloned.1.call-done = bf16[576,512]{1,0:T(8,128)(2,1)} async-done(((bf16[2304,512]{1,0:T(8,128)(2,1)}), bf16[576,512]{1,0:T(8,128)(2,1)}) %reduce-scatter.7.cloned.1.call-update) | async-done | bytes 589840
  (1 shorter events, 0.0 us)
Async XLA Ops:
  7.2 20.5 %copy-start = (bf16[1152,288]{0,1:T(8,128)(2,1)S(1)}, bf16[1152,288]{0,1:T(8,128)(2,1)}, u32[]{:S(2)}) copy-start(bf16[1152,288]{0,1:T(8,128)(2,1)} %param.9) | copy-start | bytes 1990660
  7.2 130.7 %all-gather.7.cloned.1.call-start = ((), (), s32[]{:S(2)}) async-start(), calls=%async_computation.3 | async-start | bytes 2949120 | tf_op jit(solution)/shard_map/all_gather | solution.py:49
  7.9 130.0 %all-gather.9.cloned.1.call-start = ((), (), s32[]{:S(2)}) async-start(), calls=%async_computation.4 | async-start | bytes 5971968 | tf_op jit(solution)/shard_map/all_gather | solution.py:54
  8.7 159.7 %all-gather.11.cloned.1.call-start = ((), (), s32[]{:S(2)}) async-start(), calls=%async_computation.5 | async-start | bytes 5971968 | tf_op jit(solution)/shard_map/all_gather | solution.py:53
  9.4 210.4 %all-gather.5.cloned.1.call-start = ((), (), s32[]{:S(2)}) async-start(), calls=%async_computation.2 | async-start | bytes 2949120 | tf_op jit(solution)/shard_map/all_gather | solution.py:50
  9.4 18.2 %collective-permute-start = (bf16[1152,288]{0,1:T(8,128)(2,1)}, bf16[1152,288]{0,1:T(8,128)(2,1)S(1)}, u32[]{:S(2)}, u32[]{:S(2)}) collective-permute-start(bf16[1152,288]{0,1:T(8,128)(2,1)} %param.9), channel_id=1, source_target_pairs={{0,28},{4,0},{8,4},{12,8},{16,12},{20,16},{24,20},{28,24},{1,29},{... | collective-permute-start | bytes 1990664 | tf_op jit(solution)/shard_map/ppermute | solution.py:18
  27.7 16.5 %collective-permute-start.1 = (bf16[1152,576]{0,1:T(8,128)(2,1)S(1)}, bf16[1152,576]{0,1:T(8,128)(2,1)S(1)}, u32[]{:S(2)}, u32[]{:S(2)}) collective-permute-start(bf16[1152,576]{0,1:T(8,128)(2,1)S(1)} %pad_maximum_fusion.2), channel_id=1, source_target_pairs={{0,24},{4,28},{8,0},{12,4},{16,8},{20,12},{24,16},{28,20},{1,25},{... | collective-permute-start | bytes 3981320 | tf_op jit(solution)/shard_map/ppermute | solution.py:18
  45.9 81.8 %collective-permute-start.2 = (bf16[1152,1152]{0,1:T(8,128)(2,1)}, bf16[1152,1152]{0,1:T(8,128)(2,1)}, u32[]{:S(2)}, u32[]{:S(2)}) collective-permute-start(bf16[1152,1152]{0,1:T(8,128)(2,1)} %pad_maximum_fusion.1), channel_id=1, source_target_pairs={{0,16},{4,20},{8,24},{12,28},{16,0},{20,4},{24,8},{28,12},{1,17},{... | collective-permute-start | bytes 7962632 | tf_op jit(solution)/shard_map/ppermute | solution.py:18
  46.5 347.8 %reduce-scatter.9.cloned.1.call-start = ((), (), s32[]{:S(2)}) async-start(), calls=%async_computation.7 | async-start | bytes 17915904
  137.9 30.5 %copy-start.1 = (bf16[512,2304]{0,1:T(8,128)(2,1)S(1)}, bf16[512,2304]{0,1:T(8,128)(2,1)}, u32[]{:S(2)}) copy-start(bf16[512,2304]{0,1:T(8,128)(2,1)} %all-gather.7.cloned.1.call-done) | copy-start | bytes 7077892
  219.8 6.7 %copy-start.2 = (bf16[512,2304]{0,1:T(8,128)(2,1)S(1)}, bf16[512,2304]{0,1:T(8,128)(2,1)}, u32[]{:S(2)}) copy-start(bf16[512,2304]{0,1:T(8,128)(2,1)} %all-gather.5.cloned.1.call-done) | copy-start | bytes 7077892
  219.8 6.7 %copy-start.3 = (f32[512,1152]{0,1:T(8,128)S(1)}, f32[512,1152]{0,1:T(8,128)}, u32[]{:S(2)}) copy-start(f32[512,1152]{0,1:T(8,128)} %fusion.22) | copy-start | bytes 7077892
  219.8 6.7 %copy-start.4 = (f32[512,1152]{0,1:T(8,128)S(1)}, f32[512,1152]{0,1:T(8,128)}, u32[]{:S(2)}) copy-start(f32[512,1152]{0,1:T(8,128)} %fusion.23) | copy-start | bytes 7077892
  233.8 3.2 copy-start.5
  284.2 1.3 copy-start.6
  284.3 160.5 %reduce-scatter.7.cloned.1.call-start = ((), (), s32[]{:S(2)}) async-start(), calls=%async_computation.6 | async-start | bytes 2949120
Sparse Core Ops, SparseCore 0:
  9.5 52.6 all-gather.6
  64.2 61.0 all-gather.8
  127.1 41.2 all-gather.10
  169.8 49.9 all-gather.4
  284.4 109.8 reduce-scatter.8
  397.0 47.6 reduce-scatter.6
